TPU v7x, 32 devices: a 4x4x1 block of a 4x4x8 slice. The times are simulated.
32 devices in a mesh: part: 1 (over z), loc: 4 (over y), grp: 8 (over x, core).
Axes of the slice: x: 4, y: 4, z: 1, core: 2. Of those that a mesh axis runs over, the one named last changes fastest.
The devices are a block of a 4x4x8 slice.
Arguments:
- x_tok: bfloat16 [512, 2048], P(('part', 'grp', 'loc'))
- expert_ids: int32 [512, 6], P(('part', 'grp', 'loc'))
- gate_val: float32 [512, 6], P(('part', 'grp', 'loc'))
- w_gate: bfloat16 [64, 2048, 1408], P(('grp', 'loc'))
- w_up: bfloat16 [64, 2048, 1408], P(('grp', 'loc'))
- w_down: bfloat16 [64, 1408, 2048], P(('grp', 'loc'))
Outputs:
- output: bfloat16 [512, 2048], P(('part', 'grp', 'loc'))
All inputs are finite; a program needn't handle non-finite values.
Results may differ from a plain program's by a relative error of at most 0.0117678.
Values are sent between devices in bfloat16 or wider.
A program may use at most 768 MiB of HBM per device.

v0:
```python
import jax
import jax.numpy as jnp
from jax import lax
from jax.sharding import PartitionSpec as P


def expert_rows(in_rows, row_ids, row_gate, w_gate, w_up, w_down, first_expert, capacity):
    n_rows, d_model = in_rows.shape
    top_k = row_ids.shape[1]
    n_local = w_gate.shape[0]
    local_ids = (row_ids - first_expert).reshape(-1)
    one_hot = (local_ids[:, None] == jnp.arange(n_local)[None, :]).astype(jnp.int32)
    position = jnp.sum(jnp.cumsum(one_hot, axis=0) * one_hot, axis=1) - 1
    is_valid = jnp.sum(one_hot, axis=1) > 0
    slot_ids = jnp.where(is_valid, local_ids * capacity + position, n_local * capacity)
    src_row = jnp.zeros(n_local * capacity, jnp.int32).at[slot_ids].set(jnp.arange(n_rows * top_k, dtype=jnp.int32) // top_k, mode="drop")
    src_gate = jnp.zeros(n_local * capacity, jnp.float32).at[slot_ids].set(row_gate.reshape(-1), mode="drop")
    packed = jnp.take(in_rows, src_row, axis=0).reshape(n_local, capacity, d_model)
    up_gate = jnp.einsum("ecd,edf->ecf", packed, w_gate, preferred_element_type=jnp.float32)
    up_lin = jnp.einsum("ecd,edf->ecf", packed, w_up, preferred_element_type=jnp.float32)
    hidden = (jax.nn.silu(up_gate) * up_lin).astype(jnp.bfloat16)
    out_rows = jnp.einsum("ecf,efd->ecd", hidden, w_down, preferred_element_type=jnp.float32)
    weighted = out_rows.reshape(n_local * capacity, d_model) * src_gate[:, None]
    return jax.ops.segment_sum(weighted, src_row, num_segments=n_rows)


def solution(mesh):
    n_grp = mesh.shape["grp"]
    n_loc = mesh.shape["loc"]
    tok_spec = P(("part", "grp", "loc"), None)
    w_spec = P(("grp", "loc"), None, None)

    def device_step(x_tok, expert_ids, gate_val, w_gate, w_up, w_down):
        tok_local, d_model = x_tok.shape
        top_k = expert_ids.shape[1]
        n_local = w_gate.shape[0]
        per_group = n_local * n_loc
        tokens_part = tok_local * n_grp * n_loc
        capacity = 8 * (tokens_part * top_k // (4 * per_group * n_grp) + 1)
        first_expert = (lax.axis_index("grp") * n_loc + lax.axis_index("loc")) * n_local
        owner_grp = expert_ids // per_group
        grp_mask = owner_grp[None, :, :] == jnp.arange(n_grp)[:, None, None]
        grp_hit = jnp.any(grp_mask, axis=2)
        send_rows = jnp.where(grp_hit[:, :, None], x_tok[None], jnp.zeros((), x_tok.dtype))
        send_ids = jnp.where(grp_mask, expert_ids[None], -1)
        send_gate = jnp.where(grp_mask, gate_val[None], 0.0)
        n_relay = n_grp * tok_local
        relay_rows = lax.all_to_all(send_rows, "grp", 0, 0, tiled=True).reshape(n_relay, d_model)
        relay_ids = lax.all_to_all(send_ids, "grp", 0, 0, tiled=True).reshape(n_relay, top_k)
        relay_gate = lax.all_to_all(send_gate, "grp", 0, 0, tiled=True).reshape(n_relay, top_k)
        owner_loc = (relay_ids % per_group) // n_local
        loc_mask = (owner_loc[None] == jnp.arange(n_loc)[:, None, None]) & (relay_ids >= 0)[None]
        loc_hit = jnp.any(loc_mask, axis=2)
        fan_rows = jnp.where(loc_hit[:, :, None], relay_rows[None], jnp.zeros((), relay_rows.dtype))
        fan_ids = jnp.where(loc_mask, relay_ids[None], -1)
        fan_gate = jnp.where(loc_mask, relay_gate[None], 0.0)
        got_rows = lax.all_to_all(fan_rows, "loc", 0, 0, tiled=True).reshape(n_loc * n_relay, d_model)
        got_ids = lax.all_to_all(fan_ids, "loc", 0, 0, tiled=True).reshape(n_loc * n_relay, top_k)
        got_gate = lax.all_to_all(fan_gate, "loc", 0, 0, tiled=True).reshape(n_loc * n_relay, top_k)
        row_sums = expert_rows(got_rows, got_ids, got_gate, w_gate, w_up, w_down, first_expert, capacity)
        back_sums = lax.all_to_all(row_sums.reshape(n_loc, n_relay, d_model), "loc", 0, 0, tiled=True)
        group_part = jnp.sum(back_sums, axis=0).astype(jnp.bfloat16).reshape(n_grp, tok_local, d_model)
        home_parts = lax.all_to_all(group_part, "grp", 0, 0, tiled=True)
        return jnp.sum(home_parts, axis=0, dtype=jnp.float32).astype(jnp.bfloat16)

    return jax.shard_map(device_step, mesh=mesh, in_specs=(tok_spec, tok_spec, tok_spec, w_spec, w_spec, w_spec), out_specs=tok_spec, check_vma=False)
```

profile of v0, /device:TPU:97, one launch (start us, length us, event | category | flops | bytes accessed | tf_op | source)
XLA Modules:
  0.0 177.3 jit_solution(10359256048728177152)
XLA Ops:
  0.0 0.7 add_select_fusion.3
  0.7 1.3 fusion.8
  2.0 6.0 %all-to-all-start = ((s32[8,16,6]{1,2,0:T(8,128)}), s32[8,16,6]{1,2,0:T(8,128)S(1)}, u32[]{:S(2)}, u32[]{:S(2)}) async-start(s32[8,16,6]{1,2,0:T(8,128)} %fusion.8), calls=%async_computation | async-start | bytes 65536 | tf_op jit(solution)/shard_map/all_to_all | solution.py:49
  8.0 1.3 fusion.6
  9.3 1.7 broadcast_select_fusion.4
  11.1 1.4 all-to-all-done
  12.5 4.0 %all-to-all-start.4 = ((f32[8,16,6]{1,2,0:T(8,128)}), f32[8,16,6]{1,2,0:T(8,128)S(1)}, u32[]{:S(2)}, u32[]{:S(2)}) async-start(f32[8,16,6]{1,2,0:T(8,128)} %fusion.6), calls=%async_computation.4 | async-start | bytes 65536 | tf_op jit(solution)/shard_map/all_to_all | solution.py:50
  16.6 4.4 %all-to-all-done.4 = f32[8,16,6]{1,2,0:T(8,128)S(1)} async-done(((f32[8,16,6]{1,2,0:T(8,128)}), f32[8,16,6]{1,2,0:T(8,128)S(1)}, u32[]{:S(2)}, u32[]{:S(2)}) %all-to-all-start.4) | async-done | bytes 3104 | tf_op jit(solution)/shard_map/all_to_all | solution.py:50
  21.2 0.6 fusion.15
  21.8 0.6 fusion.13
  22.4 5.6 %all-to-all-start.1 = ((s32[4,128,6]{1,2,0:T(8,128)}), s32[4,128,6]{1,2,0:T(8,128)S(1)}, u32[]{:S(2)}, u32[]{:S(2)}) async-start(s32[4,128,6]{1,2,0:T(8,128)} %fusion.15), calls=%async_computation.1 | async-start | bytes 32768 | tf_op jit(solution)/shard_map/all_to_all | solution.py:58
  28.0 4.0 %all-to-all-done.1 = s32[4,128,6]{1,2,0:T(8,128)S(1)} async-done(((s32[4,128,6]{1,2,0:T(8,128)}), s32[4,128,6]{1,2,0:T(8,128)S(1)}, u32[]{:S(2)}, u32[]{:S(2)}) %all-to-all-start.1) | async-done | bytes 12320 | tf_op jit(solution)/shard_map/all_to_all | solution.py:58
  32.0 3.3 %all-to-all-start.5 = ((f32[4,128,6]{1,2,0:T(8,128)}), f32[4,128,6]{1,2,0:T(8,128)S(1)}, u32[]{:S(2)}, u32[]{:S(2)}) async-start(f32[4,128,6]{1,2,0:T(8,128)} %fusion.13), calls=%async_computation.5 | async-start | bytes 32768 | tf_op jit(solution)/shard_map/all_to_all | solution.py:59
  35.7 3.6 %all-to-all-done.5 = f32[4,128,6]{1,2,0:T(8,128)S(1)} async-done(((f32[4,128,6]{1,2,0:T(8,128)}), f32[4,128,6]{1,2,0:T(8,128)S(1)}, u32[]{:S(2)}, u32[]{:S(2)}) %all-to-all-start.5) | async-done | bytes 12320 | tf_op jit(solution)/shard_map/all_to_all | solution.py:59
  39.3 6.7 %all-to-all-start.2 = ((bf16[8,16,2048]{2,1,0:T(8,128)(2,1)}), bf16[8,16,2048]{2,1,0:T(8,128)(2,1)S(1)}, u32[]{:S(2)}, u32[]{:S(2)}) async-start(bf16[8,16,2048]{2,1,0:T(8,128)(2,1)} %broadcast_select_fusion.4), calls=%async_computation.2 | async-start | bytes 1048576 | tf_op jit(solution)/shard_map/all_to_all | solution.py:48
  46.8 0.6 reduce-window.6
  47.6 0.2 reduce-window.9
  48.0 7.3 %all-to-all-done.2 = bf16[8,16,2048]{2,1,0:T(8,128)(2,1)S(1)} async-done(((bf16[8,16,2048]{2,1,0:T(8,128)(2,1)}), bf16[8,16,2048]{2,1,0:T(8,128)(2,1)S(1)}, u32[]{:S(2)}, u32[]{:S(2)}) %all-to-all-start.2) | async-done | bytes 524320 | tf_op jit(solution)/shard_map/all_to_all | solution.py:48
  55.2 1.6 broadcast_select_fusion
  56.8 3.7 %all-to-all-start.3 = ((bf16[4,128,2048]{2,1,0:T(8,128)(2,1)}), bf16[4,128,2048]{2,1,0:T(8,128)(2,1)S(1)}, u32[]{:S(2)}, u32[]{:S(2)}) async-start(bf16[4,128,2048]{2,1,0:T(8,128)(2,1)} %broadcast_select_fusion), calls=%async_computation.3 | async-start | bytes 4194304 | tf_op jit(solution)/shard_map/all_to_all | solution.py:57
  60.6 11.8 %scatter_custom_fusion = s32[208]{0:T(256)S(1)} fusion(s32[3072]{0:T(1024)S(1)} %bitcast.43, s32[3072]{0:T(1024)S(1)} %add_select_fusion, s32[]{:T(128)} %constant.82.clone.1), kind=kCustom, calls=%fused_computation.70 | custom fusion | bytes 836 | tf_op jit(solution)/shard_map/scatter | solution.py:16
  72.5 11.9 %scatter_custom_fusion.1 = f32[208]{0:T(256)S(1)} fusion(s32[3072]{0:T(1024)S(1)} %bitcast.44, f32[3072]{0:T(1024)S(1)} %reshape.180, f32[]{:T(128)} %constant.81.clone.1), kind=kCustom, calls=%fused_computation.68 | custom fusion | bytes 836 | tf_op jit(solution)/shard_map/scatter | solution.py:17
  84.5 1.0 all-to-all-done.3
  85.5 1.2 gather_fusion
  86.7 6.3 %fusion.3 = f32[2,104,1408]{2,1,0:T(8,128)S(1)} fusion(bf16[2,2048,1408]{2,1,0:T(8,128)(2,1)} %param.9, bf16[2,104,2048]{2,1,0:T(8,128)(2,1)S(1)} %bitcast.38, pred[2,104]{1,0:T(4,128)(4,1)S(1)} %broadcast_in_dim.144), kind=kOutput, calls=%fused_computation.11 | convolution fusion | flops 1199996928 | bytes 13557968 | tf_op jit(solution)/shard_map/ecd,edf->ecf/dot_general | solution.py:19
  93.1 6.4 %fusion = bf16[2,104,1408]{2,1,0:T(8,128)(2,1)S(1)} fusion(bf16[2,2048,1408]{2,1,0:T(8,128)(2,1)} %param.10, f32[2,104,1408]{2,1,0:T(8,128)S(1)} %fusion.3, bf16[2,104,2048]{2,1,0:T(8,128)(2,1)S(1)} %bitcast.39, pred[2,104]{1,0:T(4,128)(4,1)S(1)} %broadcast_in_dim.144), kind=kOutput, calls=%fused_computation.5 | convolution fusion | flops 1201754112 | bytes 14143696 | tf_op jit(solution)/shard_map/ecd,edf->ecf/dot_general | solution.py:20
  99.5 2.0 %fusion.30 = f32[2,104,2048]{2,1,0:T(8,128)S(1)} fusion(bf16[2,104,1408]{2,1,0:T(8,128)(2,1)S(1)} %fusion, bf16[2,1408,2048]{2,1,0:T(8,128)(2,1)S(1)} %bitcast.36), kind=kOutput, calls=%fused_computation.74 | convolution fusion | flops 1199570944 | bytes 13824000 | tf_op jit(solution)/shard_map/ecf,efd->ecd/dot_general | solution.py:22
  101.7 5.3 %scatter_custom_fusion.2 = f32[512,2048]{1,0:T(8,128)} fusion(s32[208]{0:T(256)S(1)} %scatter_custom_fusion, f32[208,2048]{1,0:T(8,128)S(1)} %bitcast_multiply_fusion, f32[]{:T(128)} %constant.81.clone.1), kind=kCustom, calls=%fused_computation.6 | custom fusion | flops 425984 | bytes 4194308 | tf_op jit(solution)/shard_map/scatter-add | solution.py:24
  107.0 51.9 %all_to_all.40 = f32[4,128,2048]{2,1,0:T(8,128)} all-to-all(f32[4,128,2048]{2,1,0:T(8,128)} %bitcast.37), channel_id=1, replica_groups=mesh['part'=1,'loc'=4,'grp'=8] {'loc'}, dimensions={0} | all-to-all | bytes 8388608 | tf_op jit(solution)/shard_map/all_to_all | solution.py:61
  158.9 2.6 %reduce_sum.41 = bf16[128,2048]{1,0:T(8,128)(2,1)S(1)} reduce(f32[4,128,2048]{2,1,0:T(8,128)} %all_to_all.40, f32[]{:T(128)} %constant.81.clone.1), dimensions={0}, to_apply=%region_9.10 | reduce | flops 786432 | bytes 4718596 | tf_op jit(solution)/shard_map/reduce_sum | solution.py:62
  161.5 15.1 %all_to_all.41 = bf16[8,16,2048]{2,1,0:T(8,128)(2,1)S(1)} all-to-all(bf16[8,16,2048]{2,1,0:T(8,128)(2,1)S(1)} %bitcast.40), channel_id=1, replica_groups=mesh['part'=1,'loc'=4,'grp'=8] {'grp'}, dimensions={0} | all-to-all | bytes 1048576 | tf_op jit(solution)/shard_map/all_to_all | solution.py:63
  176.6 0.7 reduce_sum.42
  (36 shorter events, 2.1 us)
Async XLA Ops:
  2.0 10.5 %all-to-all-start = ((s32[8,16,6]{1,2,0:T(8,128)}), s32[8,16,6]{1,2,0:T(8,128)S(1)}, u32[]{:S(2)}, u32[]{:S(2)}) async-start(s32[8,16,6]{1,2,0:T(8,128)} %fusion.8), calls=%async_computation | async-start | bytes 65536 | tf_op jit(solution)/shard_map/all_to_all | solution.py:49
  12.5 8.6 %all-to-all-start.4 = ((f32[8,16,6]{1,2,0:T(8,128)}), f32[8,16,6]{1,2,0:T(8,128)S(1)}, u32[]{:S(2)}, u32[]{:S(2)}) async-start(f32[8,16,6]{1,2,0:T(8,128)} %fusion.6), calls=%async_computation.4 | async-start | bytes 65536 | tf_op jit(solution)/shard_map/all_to_all | solution.py:50
  22.4 9.6 %all-to-all-start.1 = ((s32[4,128,6]{1,2,0:T(8,128)}), s32[4,128,6]{1,2,0:T(8,128)S(1)}, u32[]{:S(2)}, u32[]{:S(2)}) async-start(s32[4,128,6]{1,2,0:T(8,128)} %fusion.15), calls=%async_computation.1 | async-start | bytes 32768 | tf_op jit(solution)/shard_map/all_to_all | solution.py:58
  32.0 7.3 %all-to-all-start.5 = ((f32[4,128,6]{1,2,0:T(8,128)}), f32[4,128,6]{1,2,0:T(8,128)S(1)}, u32[]{:S(2)}, u32[]{:S(2)}) async-start(f32[4,128,6]{1,2,0:T(8,128)} %fusion.13), calls=%async_computation.5 | async-start | bytes 32768 | tf_op jit(solution)/shard_map/all_to_all | solution.py:59
  39.3 16.0 %all-to-all-start.2 = ((bf16[8,16,2048]{2,1,0:T(8,128)(2,1)}), bf16[8,16,2048]{2,1,0:T(8,128)(2,1)S(1)}, u32[]{:S(2)}, u32[]{:S(2)}) async-start(bf16[8,16,2048]{2,1,0:T(8,128)(2,1)} %broadcast_select_fusion.4), calls=%async_computation.2 | async-start | bytes 1048576 | tf_op jit(solution)/shard_map/all_to_all | solution.py:48
  56.8 28.7 %all-to-all-start.3 = ((bf16[4,128,2048]{2,1,0:T(8,128)(2,1)}), bf16[4,128,2048]{2,1,0:T(8,128)(2,1)S(1)}, u32[]{:S(2)}, u32[]{:S(2)}) async-start(bf16[4,128,2048]{2,1,0:T(8,128)(2,1)} %broadcast_select_fusion), calls=%async_computation.3 | async-start | bytes 4194304 | tf_op jit(solution)/shard_map/all_to_all | solution.py:57
  86.7 12.8 %slice-start = ((s8[11534336]{0:T(1024)(128)(4,1)}), s8[4194304]{0:T(1024)(128)(4,1)S(1)}, s32[]{:S(2)}) async-start(s8[11534336]{0:T(1024)(128)(4,1)} %bitcast.35), calls=%async_computation.8 | async-start | bytes 8388608
  86.7 12.8 %slice-start.1 = ((s8[11534336]{0:T(1024)(128)(4,1)}), s8[4194304]{0:T(1024)(128)(4,1)S(1)}, s32[]{:S(2)}) async-start(s8[11534336]{0:T(1024)(128)(4,1)} %bitcast.35), calls=%async_computation.9 | async-start | bytes 8388608
  93.1 6.5 %slice-start.2 = ((s8[11534336]{0:T(1024)(128)(4,1)}), s8[3145728]{0:T(1024)(128)(4,1)S(1)}, s32[]{:S(2)}) async-start(s8[11534336]{0:T(1024)(128)(4,1)} %bitcast.35), calls=%async_computation.10 | async-start | bytes 6291456
where the time goes:
time: 178 us; the launch traced here: 177 us
  blocking collectives  67 us (38%)
  starting transfers between devices  29.4 us (17%)
  local copies, waits for them, and re-layouts  26.5 us (15%)
  waiting for transfers between devices  21.7 us (12%)
  other arithmetic  17.7 us (10%)
  matrix products  14.8 us (8%)
    all_to_all x1, blocking collectives, device_step(): lax.all_to_all(row_sums.reshape(n_loc, n_relay, d_model), 'loc', 0, 0, ti...  51.9 us
    all_to_all x1, blocking collectives, device_step(): home_parts = lax.all_to_all(group_part, 'grp', 0, 0, tiled=True)  15.1 us
    scatter x1, local copies, waits for them, and re-layouts, expert_rows(): jnp.zeros(n_local * capacity, jnp.float32).at[slot_ids]  11.9 us
    scatter x1, local copies, waits for them, and re-layouts, expert_rows(): jnp.zeros(n_local * capacity, jnp.int32).at[slot_ids]  11.8 us
    all_to_all x1, waiting for transfers between devices, device_step(): lax.all_to_all(send_rows, 'grp', 0, 0, tiled=True).reshape(n_relay, d_model)  7.26 us
    all_to_all x1, starting transfers between devices, device_step(): lax.all_to_all(send_rows, 'grp', 0, 0, tiled=True).reshape(n_relay, d_model)  6.72 us
    dot_general x1, matrix products, expert_rows(): jnp.einsum('ecd,edf->ecf', packed, w_up, preferred_element_type=jnp.float32)  6.42 us
    dot_general x1, matrix products, expert_rows(): jnp.einsum('ecd,edf->ecf', packed, w_gate, preferred_element_type=jnp.flo...  6.34 us
  transfers between devices with their start and end apart: 6, of which 6 were waited for; matrix products, arithmetic and copies ran while one was open for 17% of the time, Pallas kernels for 0%

commit v1 on v0

v1 whole, which is shorter than its diff:
```python
import functools

import jax
import jax.numpy as jnp
from jax import lax
from jax.experimental import pallas as pl
from jax.experimental.pallas import tpu as pltpu
from jax.sharding import PartitionSpec as P

MESH = pl.DeviceIdType.MESH
F32, BF16 = jnp.float32, jnp.bfloat16
N_SUB = 2


def remote(src, dst, send_sem, recv_sem, device):
    return pltpu.make_async_remote_copy(src_ref=src, dst_ref=dst, send_sem=send_sem, recv_sem=recv_sem, device_id=device, device_id_type=MESH)


def layer_kernel(n_loc, n_grp, cap, top_k, x_ref, ids_ref, gate_ref, wg_hbm, wu_hbm, wd_hbm, out_ref,
                 wg, wu, wd, xall, mall, xg, hid, combine, ysend, yrecv, gpart, grecv, fin, frecv,
                 w_sem, m_send, m_recv, a_send, a_recv, b_send, b_recv, s_send, s_recv,
                 y_send, y_recv, g_send, g_recv, f_send, f_recv):
    n_x = n_grp // 2
    tok, d_model = x_ref.shape
    half = d_model // 2
    n_exp, _, d_ff = wg.shape
    per_group = n_exp * n_loc
    quarter = d_model // n_loc
    sub = quarter // N_SUB
    n_tok = n_grp * n_loc * tok
    slot_pad = yrecv.shape[2]

    l, g = lax.axis_index("loc"), lax.axis_index("grp")
    gx, gc = g // 2, g % 2

    def at_y(d):
        return (l + d + n_loc) % n_loc

    def at_x(d):
        return (gx + d + n_x) % n_x

    def at_g(d):
        return (g + d + n_grp) % n_grp

    def dev_y(d):
        return {"loc": at_y(d), "grp": g}

    def dev_x(d):
        return {"loc": l, "grp": at_x(d) * 2 + gc}

    def dev_g(d):
        return {"loc": l, "grp": at_g(d)}

    sibling = {"loc": l, "grp": gx * 2 + 1 - gc}

    loads = {}
    for e in range(n_exp):
        for j, (src, dst) in enumerate(((wg_hbm, wg), (wu_hbm, wu))):
            loads[e, j] = pltpu.make_async_copy(src.at[e], dst.at[e], w_sem.at[e, j])
            loads[e, j].start()
        for d in (2, 1, 3, 0):
            cols = pl.ds(pl.multiple_of(at_y(d) * quarter, quarter), quarter)
            loads[e, 2 + d] = pltpu.make_async_copy(wd_hbm.at[e, :, cols], wd.at[e, d], w_sem.at[e, 2 + d])
            loads[e, 2 + d].start()

    mall[gx, gc, l] = jnp.zeros(mall.shape[3:], F32)
    mall[gx, gc, l, :, 0:top_k] = ids_ref[...].astype(F32)
    mall[gx, gc, l, :, 8:8 + top_k] = gate_ref[...]
    xall[0, gx, gc, l] = x_ref[:, 0:half]
    xall[1, gx, gc, l] = x_ref[:, half:]

    barrier = pltpu.get_barrier_semaphore()
    for d in range(1, n_loc):
        pl.semaphore_signal(barrier, inc=1, device_id=dev_y(d), device_id_type=MESH)
    for d in range(1, n_grp):
        pl.semaphore_signal(barrier, inc=1, device_id=dev_g(d), device_id_type=MESH)
    pl.semaphore_wait(barrier, n_loc + n_grp - 2)

    sent = []

    def go(copy):
        copy.start()
        sent.append(copy)
        return copy

    m1 = [go(remote(mall.at[gx, gc, l], mall.at[gx, gc, l], m_send.at[d], m_recv.at[d], dev_y(d))) for d in range(1, n_loc)]
    a0 = [go(remote(x_ref.at[:, 0:half], xall.at[0, gx, gc, l], a_send.at[0, d], a_recv.at[0, d], dev_y(d))) for d in (2, 1, 3)]
    a1 = [go(remote(x_ref.at[:, half:d_model], xall.at[1, gx, gc, l], a_send.at[1, d], a_recv.at[1, d], dev_x(d))) for d in (2, 1, 3)]

    yrecv[:, :, cap:, :] = jnp.zeros((N_SUB, 2 * n_loc, slot_pad - cap, sub), F32)

    for c in m1:
        c.wait_recv()
    m2 = [go(remote(mall.at[gx, gc], mall.at[gx, gc], m_send.at[4 + d], m_recv.at[4 + d], dev_x(d))) for d in range(1, n_x)]
    ms = [go(remote(mall.at[gx, gc], mall.at[gx, gc], m_send.at[8], m_recv.at[8], sibling))]
    for c in a0:
        c.wait_recv()
    b0 = {d: go(remote(xall.at[0, gx, gc], xall.at[0, gx, gc], b_send.at[0, d], b_recv.at[0, d], dev_x(d))) for d in (2, 1, 3)}
    for c in a1:
        c.wait_recv()
    b1 = {d: go(remote(xall.at[1, :, gc, l], xall.at[1, :, gc, l], b_send.at[1, d], b_recv.at[1, d], dev_y(d))) for d in (2, 1, 3)}
    sib = [go(remote(xall.at[0, gx, gc], xall.at[0, gx, gc], s_send.at[0, 0], s_recv.at[0, 0], sibling))]
    sib.append(go(remote(xall.at[1, :, gc, l], xall.at[1, :, gc, l], s_send.at[1, 0], s_recv.at[1, 0], sibling)))
    for d in range(1, n_x):
        m2[d - 1].wait_recv()
        part = mall.at[at_x(-d), gc]
        ms.append(go(remote(part, part, m_send.at[8 + d], m_recv.at[8 + d], sibling)))
    for c in ms:
        c.wait_recv()

    meta = mall[...].reshape(n_tok, mall.shape[-1])
    lane = lax.broadcasted_iota(jnp.int32, meta.shape, 1)
    lane_exp = g * per_group + ((l + n_loc - lane // n_exp) % n_loc) * n_exp + lane % n_exp
    lane_exp = jnp.where(lane < per_group, lane_exp, -1).astype(F32)
    member = jnp.zeros(meta.shape, F32)
    gates = jnp.zeros(meta.shape, F32)
    for j in range(top_k):
        same = meta[:, j:j + 1] == lane_exp
        member = jnp.where(same, 1.0, member)
        gates = jnp.where(same, meta[:, 8 + j:9 + j], gates)
    tri_r = lax.broadcasted_iota(jnp.int32, (n_tok, n_tok), 0)
    tri_c = lax.broadcasted_iota(jnp.int32, (n_tok, n_tok), 1)
    before = jnp.dot(jnp.where(tri_c < tri_r, 1.0, 0.0).astype(BF16), member.astype(BF16), preferred_element_type=F32)
    slot = jnp.where(member > 0.0, before, -1.0)
    slot_lane = lax.broadcasted_iota(jnp.int32, (n_tok, slot_pad), 1).astype(F32)
    for b in range(per_group):
        combine[:, b * slot_pad:(b + 1) * slot_pad] = jnp.where(slot_lane == slot[:, b:b + 1], 1.0, 0.0).astype(BF16)
    slot_rows = jnp.transpose(slot)
    gate_rows = jnp.transpose(gates)
    cap_row = lax.broadcasted_iota(jnp.int32, (cap, n_tok), 0).astype(F32)
    picks, slot_gate = [], []
    for e in range(n_exp):
        hit = cap_row == slot_rows[e:e + 1, :]
        picks.append(jnp.where(hit, 1.0, 0.0).astype(BF16))
        slot_gate.append(jnp.sum(jnp.where(hit, gate_rows[e:e + 1, :], 0.0), axis=1, keepdims=True))

    for d in (1, 3, 2):
        b0[d].wait_recv()
        part = xall.at[0, at_x(-d), gc]
        sib.append(go(remote(part, part, s_send.at[0, d], s_recv.at[0, d], sibling)))
        b1[d].wait_recv()
        part = xall.at[1, :, gc, at_y(-d)]
        sib.append(go(remote(part, part, s_send.at[1, d], s_recv.at[1, d], sibling)))
    for c in sib:
        c.wait_recv()

    for e in range(n_exp):
        for h in range(2):
            rows = xall[h].reshape(n_tok, half)
            xg[e, :, h * half:(h + 1) * half] = jnp.dot(picks[e], rows, preferred_element_type=F32).astype(BF16)

    y_copies = {}
    for e in range(n_exp):
        loads[e, 0].wait()
        loads[e, 1].wait()
        rows = xg[e]
        tile = min(256, d_ff)
        for c0 in range(0, d_ff, tile):
            c1 = min(d_ff, c0 + tile)
            u = jnp.dot(rows, wg[e, :, c0:c1], preferred_element_type=F32)
            v = jnp.dot(rows, wu[e, :, c0:c1], preferred_element_type=F32)
            hid[e, :, c0:c1] = (jax.nn.silu(u) * v).astype(BF16)
        for d in (2, 1, 3):
            loads[e, 2 + d].wait()
            o = jnp.dot(hid[e], wd[e, d], preferred_element_type=F32) * slot_gate[e]
            for k in range(N_SUB):
                ysend[d - 1, e, k] = o[:, k * sub:(k + 1) * sub]
        for k in range(N_SUB):
            for d in (2, 1, 3):
                y_copies[e, k, d] = go(remote(ysend.at[d - 1, e, k], yrecv.at[k, n_exp * d + e, pl.ds(0, cap)], y_send.at[e, k, d], y_recv.at[e, k, d], dev_y(d)))
    for e in range(n_exp):
        loads[e, 2].wait()
        o = jnp.dot(hid[e], wd[e, 0], preferred_element_type=F32) * slot_gate[e]
        for k in range(N_SUB):
            yrecv[k, e, 0:cap, :] = o[:, k * sub:(k + 1) * sub]

    g_copies = {}
    for k in range(N_SUB):
        for e in range(n_exp):
            for d in (1, 3, 2):
                y_copies[e, k, d].wait_recv()
        vals = yrecv[k].reshape(per_group * slot_pad, sub)
        hi = vals.astype(BF16)
        rest = vals - hi.astype(F32)
        mid = rest.astype(BF16)
        low = (rest - mid.astype(F32)).astype(BF16)
        sel = combine[...]
        acc = jnp.dot(sel, hi, preferred_element_type=F32)
        acc += jnp.dot(sel, mid, preferred_element_type=F32)
        acc += jnp.dot(sel, low, preferred_element_type=F32)
        gpart[k] = acc.astype(BF16).reshape(n_grp, n_loc * tok, sub)
        for d in (4, 3, 5, 2, 6, 1, 7):
            g_copies[k, d] = go(remote(gpart.at[k, at_g(d)], grecv.at[k, d], g_send.at[k, d], g_recv.at[k, d], dev_g(d)))

    f_copies = {}
    for k in range(N_SUB):
        total = gpart[k, g].astype(F32)
        for d in range(1, n_grp):
            g_copies[k, d].wait_recv()
            total += grecv[k, d].astype(F32)
        fin[k] = total.astype(BF16).reshape(n_loc, tok, sub)
        for d in (2, 1, 3):
            f_copies[k, d] = go(remote(fin.at[k, at_y(d)], frecv.at[k, d], f_send.at[k, d], f_recv.at[k, d], dev_y(d)))
    for k in range(N_SUB):
        for d in range(n_loc):
            if d:
                f_copies[k, d].wait_recv()
            cols = pl.ds(pl.multiple_of(at_y(-d) * quarter + k * sub, sub), sub)
            out_ref[:, cols] = frecv[k, d] if d else fin[k, l]
    for c in sent:
        c.wait_send()


def solution(mesh):
    n_grp, n_loc = mesh.shape["grp"], mesh.shape["loc"]
    tok_spec = P(("part", "grp", "loc"), None)
    w_spec = P(("grp", "loc"), None, None)

    def device_step(x_tok, expert_ids, gate_val, w_gate, w_up, w_down):
        tok, d_model = x_tok.shape
        top_k = expert_ids.shape[1]
        n_exp, _, d_ff = w_gate.shape
        n_tok = tok * n_grp * n_loc
        cap = 8 * (n_tok * top_k // (4 * n_exp * n_loc * n_grp) + 1)
        slot_pad = -(-cap // 128) * 128
        quarter = d_model // n_loc
        sub = quarter // N_SUB
        dma = pltpu.SemaphoreType.DMA
        vmem = pl.BlockSpec(memory_space=pltpu.VMEM)
        hbm = pl.BlockSpec(memory_space=pl.ANY)
        return pl.pallas_call(
            functools.partial(layer_kernel, n_loc, n_grp, cap, top_k),
            out_shape=jax.ShapeDtypeStruct((tok, d_model), BF16),
            in_specs=[vmem, vmem, vmem, hbm, hbm, hbm],
            out_specs=vmem,
            scratch_shapes=[
                pltpu.VMEM((n_exp, d_model, d_ff), BF16),
                pltpu.VMEM((n_exp, d_model, d_ff), BF16),
                pltpu.VMEM((n_exp, n_loc, d_ff, quarter), BF16),
                pltpu.VMEM((2, n_grp // 2, 2, n_loc, tok, d_model // 2), BF16),
                pltpu.VMEM((n_grp // 2, 2, n_loc, tok, 128), F32),
                pltpu.VMEM((n_exp, cap, d_model), BF16),
                pltpu.VMEM((n_exp, cap, d_ff), BF16),
                pltpu.VMEM((n_tok, n_exp * n_loc * slot_pad), BF16),
                pltpu.VMEM((n_loc - 1, n_exp, N_SUB, cap, sub), F32),
                pltpu.VMEM((N_SUB, n_exp * n_loc, slot_pad, sub), F32),
                pltpu.VMEM((N_SUB, n_grp, n_loc * tok, sub), BF16),
                pltpu.VMEM((N_SUB, n_grp, n_loc * tok, sub), BF16),
                pltpu.VMEM((N_SUB, n_loc, tok, sub), BF16),
                pltpu.VMEM((N_SUB, n_loc, tok, sub), BF16),
                dma((n_exp, 2 + n_loc)),
                dma((12,)), dma((12,)),
                dma((2, 4)), dma((2, 4)),
                dma((2, 4)), dma((2, 4)),
                dma((2, 4)), dma((2, 4)),
                dma((n_exp, N_SUB, n_loc)), dma((n_exp, N_SUB, n_loc)),
                dma((N_SUB, n_grp)), dma((N_SUB, n_grp)),
                dma((N_SUB, n_loc)), dma((N_SUB, n_loc)),
            ],
            compiler_params=pltpu.CompilerParams(collective_id=0, has_side_effects=True, vmem_limit_bytes=64000 * 1024),
        )(x_tok, expert_ids, gate_val, w_gate, w_up, w_down)

    return jax.shard_map(device_step, mesh=mesh, in_specs=(tok_spec, tok_spec, tok_spec, w_spec, w_spec, w_spec), out_specs=tok_spec, check_vma=False)
```

time: 178 us -> 62.8 us (0.35)
  blocking collectives: 67 us -> 0 us
  Pallas kernels: 0 us -> 58.3 us
  starting transfers between devices: 29.4 us -> 0 us
  local copies, waits for them, and re-layouts: 26.5 us -> 4.19 us
  waiting for transfers between devices: 21.7 us -> 0 us
  other arithmetic: 17.7 us -> 0 us
  matrix products: 14.8 us -> 0 us
    all_to_all x2 -> x0, blocking collectives: 67 us -> none  [the longest x1 51.9 us: device_step(): lax.all_to_all(row_sums.reshape(n_loc, n_relay, d_model), 'loc', 0, 0, ti...]
    pallas_call x0 -> x1, Pallas kernels: none -> 58.3 us  [device_step(): pl.pallas_call(functools.partial(layer_kernel, n_loc, n_grp, cap, top_k),...]
    all_to_all x6 -> x0, starting transfers between devices: 29.4 us -> none  [the longest x1 6.72 us: device_step(): lax.all_to_all(send_rows, 'grp', 0, 0, tiled=True).reshape(n_relay, d_model)]
    scatter x2 -> x0, local copies, waits for them, and re-layouts: 23.7 us -> none  [the longest x1 11.9 us: expert_rows(): jnp.zeros(n_local * capacity, jnp.float32).at[slot_ids]]
    all_to_all x6 -> x0, waiting for transfers between devices: 21.7 us -> none  [the longest x1 7.26 us: device_step(): lax.all_to_all(send_rows, 'grp', 0, 0, tiled=True).reshape(n_relay, d_model)]
    dot_general x3 -> x0, matrix products: 14.8 us -> none  [the longest x1 6.42 us: expert_rows(): jnp.einsum('ecd,edf->ecf', packed, w_up, preferred_element_type=jnp.float32)]
    select_n x11 -> x0, other arithmetic: 7.9 us -> none  [the longest x1 1.73 us: device_step(): jnp.where(grp_hit[:, :, None], x_tok[None], jnp.zeros((), x_tok.dtype))]
    scatter-add x1 -> x0, other arithmetic: 5.26 us -> none  [expert_rows(): return jax.ops.segment_sum(weighted, src_row, num_segments=n_rows)]
  transfers between devices with their start and end apart: 6 -> 0, of which waited for: 6 -> 0; matrix products, arithmetic and copies ran while one was open for 17% -> 0% of each run, Pallas kernels for 0% -> 0%
where the time goes in v1:
time: 62.8 us; the launch traced here: 62.5 us
  Pallas kernels  58.3 us (93%)
  local copies, waits for them, and re-layouts  4.19 us (7%)
    pallas_call x1, Pallas kernels, device_step(): pl.pallas_call(functools.partial(layer_kernel, n_loc, n_grp, cap, top_k),...  58.3 us
    unnamed x3, local copies, waits for them, and re-layouts  4.19 us

profile of v1, /device:TPU:97, one launch (start us, length us, event | category | flops | bytes accessed | tf_op | source)
XLA Modules:
  0.0 62.5 jit_solution(1680324055347873371)
XLA Ops:
  0.0 1.4 %copy.7.ids_ref = s32[16,6]{1,0:T(8,128)} copy(s32[16,6]{0,1:T(8,128)} %param.7) | data formatting | bytes 768 | tf_op args[1]
  1.4 1.4 %copy.8.gate_ref = f32[16,6]{1,0:T(8,128)} copy(f32[16,6]{0,1:T(8,128)} %param.8) | data formatting | bytes 768 | tf_op args[2]
  2.7 58.3 %shard_map.64 = bf16[16,2048]{1,0:T(8,128)(2,1)} custom-call(bf16[16,2048]{1,0:T(8,128)(2,1)} %x_ref.1, s32[16,6]{1,0:T(8,128)} %copy.7.ids_ref, f32[16,6]{1,0:T(8,128)} %copy.8.gate_ref, bf16[2,2048,1408]{2,1,0:T(8,128)(2,1)} %wg_hbm.1, bf16[2,2048,1408]{2,1,0:T(8,128)(2,1)} %wu_hbm.1, bf16[2,1408,2048]{2,1,0:T(8,128)(2,1)} %wd_hbm.1), custom_call_target="tpu_custom_call" | custom-call | tf_op jit(solution)/shard_map/pallas_call | solution.py:231
  61.1 1.5 %copy.10 = bf16[16,2048]{1,0:T(8,128)(2,1)} copy(bf16[16,2048]{1,0:T(8,128)(2,1)} %shard_map.64) | data formatting | bytes 131072

commit v2 on v1

v2 whole, which is shorter than its diff:
```python
import functools

import jax
import jax.numpy as jnp
from jax import lax
from jax.experimental import pallas as pl
from jax.experimental.pallas import tpu as pltpu
from jax.sharding import PartitionSpec as P

MESH = pl.DeviceIdType.MESH
F32, BF16 = jnp.float32, jnp.bfloat16
N_SUB = 4
N_CHUNK = 4


def remote(src, dst, send_sem, recv_sem, device):
    return pltpu.make_async_remote_copy(src_ref=src, dst_ref=dst, send_sem=send_sem, recv_sem=recv_sem, device_id=device, device_id_type=MESH)


def layer_kernel(n_loc, n_grp, cap, top_k, x_ref, ids_ref, gate_ref, wg_hbm, wu_hbm, wd_hbm, out_ref,
                 wg, wu, wd, xall, mown, mcol, mrow, mall, tri, picks, xg, uacc, vacc, hid, combine, ysend, yrecv, gpart, grecv, fin, frecv,
                 w_sem, m_send, m_recv, r_send, r_recv, a_send, a_recv, b_send, b_recv, s_send, s_recv,
                 y_send, y_recv, g_send, g_recv, f_send, f_recv):
    n_x = n_grp // 2
    tok, d_model = x_ref.shape
    width = d_model // N_CHUNK
    n_exp, _, d_ff = wg.shape
    per_group = n_exp * n_loc
    quarter = d_model // n_loc
    sub = quarter // N_SUB
    n_tok = n_grp * n_loc * tok
    slot_pad = yrecv.shape[2]
    cap_pad = hid.shape[1]

    l, g = lax.axis_index("loc"), lax.axis_index("grp")
    gx, gc = g // 2, g % 2

    def at_y(d):
        return (l + d + n_loc) % n_loc

    def at_x(d):
        return (gx + d + n_x) % n_x

    def at_g(d):
        return (g + d + n_grp) % n_grp

    def dev_y(d):
        return {"loc": at_y(d), "grp": g}

    def dev_x(d):
        return {"loc": l, "grp": at_x(d) * 2 + gc}

    def dev_g(d):
        return {"loc": l, "grp": at_g(d)}

    sibling = {"loc": l, "grp": gx * 2 + 1 - gc}

    barrier = pltpu.get_barrier_semaphore()
    for d in range(1, n_loc):
        pl.semaphore_signal(barrier, inc=1, device_id=dev_y(d), device_id_type=MESH)
    for d in range(1, n_grp):
        pl.semaphore_signal(barrier, inc=1, device_id=dev_g(d), device_id_type=MESH)

    loads = {}
    for e in range(n_exp):
        for j, (src, dst) in enumerate(((wg_hbm, wg), (wu_hbm, wu))):
            loads[e, j] = pltpu.make_async_copy(src.at[e], dst.at[e], w_sem.at[e, j])
            loads[e, j].start()
    for e in range(n_exp):
        for d in (2, 1, 3, 0):
            cols = pl.ds(pl.multiple_of(at_y(d) * quarter, quarter), quarter)
            loads[e, 2 + d] = pltpu.make_async_copy(wd_hbm.at[e, :, cols], wd.at[e, d], w_sem.at[e, 2 + d])
            loads[e, 2 + d].start()

    mown[...] = jnp.zeros(mown.shape, F32)
    mown[0:top_k, 0:tok] = ids_ref[...].astype(F32)
    mown[8:8 + top_k, 0:tok] = gate_ref[...]
    mown[...] = pltpu.roll(mown[...], gc * (n_loc * tok) + l * tok, 1)
    for h in range(N_CHUNK):
        xall[h, gx, gc, l] = x_ref[:, h * width:(h + 1) * width]
    tri_r = lax.broadcasted_iota(jnp.int32, (n_tok, n_tok), 0)
    tri_c = lax.broadcasted_iota(jnp.int32, (n_tok, n_tok), 1)
    tri[...] = jnp.where(tri_r < tri_c, 1.0, 0.0).astype(BF16)
    yrecv[:, :, cap:, :] = jnp.zeros((N_SUB, per_group, slot_pad - cap, sub), F32)

    pl.semaphore_wait(barrier, n_loc + n_grp - 2)

    sent = []

    def go(copy):
        copy.start()
        sent.append(copy)
        return copy

    far_first, near_first = (2, 1, 3), (1, 3, 2)
    m1 = [go(remote(mown, mcol.at[d], m_send.at[d], m_recv.at[d], dev_y(d))) for d in far_first]
    a = {}
    for h in range(N_CHUNK):
        for d in far_first:
            a[h, d] = go(remote(x_ref.at[:, h * width:(h + 1) * width], xall.at[h, gx, gc, l], a_send.at[h, d], a_recv.at[h, d], dev_x(d) if h % 2 else dev_y(d)))
    for c in m1:
        c.wait_recv()
    mrow[...] = mown[...] + mcol[1] + mcol[2] + mcol[3]
    mall[g] = mrow[...]
    m2 = [go(remote(mrow, mall.at[g], r_send.at[d], r_recv.at[d], dev_g(d))) for d in range(1, n_grp)]

    def region(h, d):
        return xall.at[h, :, gc, at_y(-d)] if h % 2 else xall.at[h, at_x(-d), gc]

    b, sib = {}, {}

    def relay(h, d):
        sib[h, d] = go(remote(region(h, d), region(h, d), s_send.at[h, d], s_recv.at[h, d], sibling))

    for h in range(N_CHUNK):
        for d in near_first:
            a[h, d].wait_recv()
        for d in far_first:
            b[h, d] = go(remote(region(h, 0), region(h, 0), b_send.at[h, d], b_recv.at[h, d], dev_y(d) if h % 2 else dev_x(d)))
        relay(h, 0)

    for c in m2:
        c.wait_recv()
    meta = jnp.concatenate([mall[2 * i] + mall[2 * i + 1] for i in range(n_x)], axis=1)
    row = lax.broadcasted_iota(jnp.int32, (per_group, n_tok), 0)
    row_exp = (g * per_group + ((l + n_loc - row // n_exp) % n_loc) * n_exp + row % n_exp).astype(F32)
    member = jnp.zeros(row.shape, F32)
    gates = jnp.zeros(row.shape, F32)
    for j in range(top_k):
        same = meta[j:j + 1, :] == row_exp
        member = jnp.where(same, 1.0, member)
        gates = jnp.where(same, meta[8 + j:9 + j, :], gates)
    before = jnp.dot(member.astype(BF16), tri[...], preferred_element_type=F32)
    slot = jnp.where(member > 0.0, before, -1.0)
    cap_row = lax.broadcasted_iota(jnp.int32, (cap_pad, n_tok), 0).astype(F32)
    slot_gate = []
    for e in range(n_exp):
        hit = cap_row == slot[e:e + 1, :]
        picks[e * cap_pad:(e + 1) * cap_pad, :] = jnp.where(hit, 1.0, 0.0).astype(BF16)
        slot_gate.append(jnp.sum(jnp.where(hit, gates[e:e + 1, :], 0.0), axis=1, keepdims=True))

    tile = min(256, d_ff)
    tiles = [(c0, min(d_ff, c0 + tile)) for c0 in range(0, d_ff, tile)]
    for p in range(N_CHUNK // 2):
        pair = (2 * p, 2 * p + 1)
        for d in near_first:
            for h in pair:
                b[h, d].wait_recv()
                relay(h, d)
        for h in pair:
            for d in (0,) + near_first:
                sib[h, d].wait_recv()
        for h in pair:
            rows = xall[h].reshape(n_tok, width)
            got = jnp.dot(picks[...], rows, preferred_element_type=F32).astype(BF16)
            for e in range(n_exp):
                xg[e, :, h * width:(h + 1) * width] = got[e * cap_pad:(e + 1) * cap_pad]
        k0, k1 = 2 * p * width, 2 * (p + 1) * width
        if p == 0:
            for e in range(n_exp):
                loads[e, 0].wait()
                loads[e, 1].wait()
                for c0, c1 in tiles:
                    uacc[e, :, c0:c1] = jnp.dot(xg[e, :, k0:k1], wg[e, k0:k1, c0:c1], preferred_element_type=F32)
                    vacc[e, :, c0:c1] = jnp.dot(xg[e, :, k0:k1], wu[e, k0:k1, c0:c1], preferred_element_type=F32)
    y_copies = {}
    for e in range(n_exp):
        for c0, c1 in tiles:
            u = uacc[e, :, c0:c1] + jnp.dot(xg[e, :, k0:k1], wg[e, k0:k1, c0:c1], preferred_element_type=F32)
            v = vacc[e, :, c0:c1] + jnp.dot(xg[e, :, k0:k1], wu[e, k0:k1, c0:c1], preferred_element_type=F32)
            hid[e, :, c0:c1] = (jax.nn.silu(u) * v).astype(BF16)

        def send_rows(e, k, d):
            y_copies[e, k, d] = go(remote(ysend.at[d - 1, e, k, pl.ds(0, cap)], yrecv.at[k, n_exp * d + e, pl.ds(0, cap)], y_send.at[e, k, d], y_recv.at[e, k, d], dev_y(d)))

        for d in far_first:
            loads[e, 2 + d].wait()
            o = jnp.dot(hid[e], wd[e, d], preferred_element_type=F32) * slot_gate[e]
            for k in range(N_SUB):
                ysend[d - 1, e, k] = o[:, k * sub:(k + 1) * sub]
            if e + 1 < n_exp:
                for k in range(N_SUB):
                    send_rows(e, k, d)
        if e + 1 == n_exp:
            for k in range(N_SUB):
                for d in far_first:
                    send_rows(e, k, d)
    for e in range(n_exp):
        loads[e, 2].wait()
        o = jnp.dot(hid[e], wd[e, 0], preferred_element_type=F32) * slot_gate[e]
        for k in range(N_SUB):
            yrecv[k, e, 0:cap, :] = o[0:cap, k * sub:(k + 1) * sub]
    slot_cols = jnp.transpose(jnp.concatenate([slot, jnp.zeros((128 - per_group, n_tok), F32)], axis=0))
    slot_lane = lax.broadcasted_iota(jnp.int32, (n_tok, slot_pad), 1).astype(F32)
    for i in range(per_group):
        combine[:, i * slot_pad:(i + 1) * slot_pad] = jnp.where(slot_lane == slot_cols[:, i:i + 1], 1.0, 0.0).astype(BF16)

    g_copies = {}
    for k in range(N_SUB):
        for e in range(n_exp):
            for d in near_first:
                y_copies[e, k, d].wait_recv()
        vals = yrecv[k].reshape(per_group * slot_pad, sub)
        hi = vals.astype(BF16)
        rest = vals - hi.astype(F32)
        mid = rest.astype(BF16)
        low = (rest - mid.astype(F32)).astype(BF16)
        sel = combine[...]
        acc = jnp.dot(sel, hi, preferred_element_type=F32)
        acc += jnp.dot(sel, mid, preferred_element_type=F32)
        acc += jnp.dot(sel, low, preferred_element_type=F32)
        gpart[k] = acc.astype(BF16).reshape(n_grp, n_loc * tok, sub)
        for d in (4, 3, 5, 2, 6, 1, 7):
            g_copies[k, d] = go(remote(gpart.at[k, at_g(d)], grecv.at[k, d], g_send.at[k, d], g_recv.at[k, d], dev_g(d)))

    f_copies = {}
    for k in range(N_SUB):
        total = gpart[k, g].astype(F32)
        for d in range(1, n_grp):
            g_copies[k, d].wait_recv()
            total += grecv[k, d].astype(F32)
        fin[k] = total.astype(BF16).reshape(n_loc, tok, sub)
        for d in far_first:
            f_copies[k, d] = go(remote(fin.at[k, at_y(d)], frecv.at[k, d], f_send.at[k, d], f_recv.at[k, d], dev_y(d)))
    for k in range(N_SUB):
        for d in range(n_loc):
            if d:
                f_copies[k, d].wait_recv()
            cols = pl.ds(pl.multiple_of(at_y(-d) * quarter + k * sub, sub), sub)
            out_ref[:, cols] = frecv[k, d] if d else fin[k, l]
    for c in sent:
        c.wait_send()


def solution(mesh):
    n_grp, n_loc = mesh.shape["grp"], mesh.shape["loc"]
    tok_spec = P(("part", "grp", "loc"), None)
    w_spec = P(("grp", "loc"), None, None)

    def device_step(x_tok, expert_ids, gate_val, w_gate, w_up, w_down):
        tok, d_model = x_tok.shape
        top_k = expert_ids.shape[1]
        n_exp, _, d_ff = w_gate.shape
        n_tok = tok * n_grp * n_loc
        per_group = n_exp * n_loc
        cap = 8 * (n_tok * top_k // (4 * per_group * n_grp) + 1)
        slot_pad = -(-cap // 128) * 128
        cap_pad = -(-cap // 16) * 16
        quarter = d_model // n_loc
        sub = quarter // N_SUB
        dma = pltpu.SemaphoreType.DMA
        vmem = pl.BlockSpec(memory_space=pltpu.VMEM)
        hbm = pl.BlockSpec(memory_space=pl.ANY)
        return pl.pallas_call(
            functools.partial(layer_kernel, n_loc, n_grp, cap, top_k),
            out_shape=jax.ShapeDtypeStruct((tok, d_model), BF16),
            in_specs=[vmem, vmem, vmem, hbm, hbm, hbm],
            out_specs=vmem,
            scratch_shapes=[
                pltpu.VMEM((n_exp, d_model, d_ff), BF16),
                pltpu.VMEM((n_exp, d_model, d_ff), BF16),
                pltpu.VMEM((n_exp, n_loc, d_ff, quarter), BF16),
                pltpu.VMEM((N_CHUNK, n_grp // 2, 2, n_loc, tok, d_model // N_CHUNK), BF16),
                pltpu.VMEM((16, 128), F32),
                pltpu.VMEM((n_loc, 16, 128), F32),
                pltpu.VMEM((16, 128), F32),
                pltpu.VMEM((n_grp, 16, 128), F32),
                pltpu.VMEM((n_tok, n_tok), BF16),
                pltpu.VMEM((n_exp * cap_pad, n_tok), BF16),
                pltpu.VMEM((n_exp, cap_pad, d_model), BF16),
                pltpu.VMEM((n_exp, cap_pad, d_ff), F32),
                pltpu.VMEM((n_exp, cap_pad, d_ff), F32),
                pltpu.VMEM((n_exp, cap_pad, d_ff), BF16),
                pltpu.VMEM((n_tok, per_group * slot_pad), BF16),
                pltpu.VMEM((n_loc - 1, n_exp, N_SUB, cap_pad, sub), F32),
                pltpu.VMEM((N_SUB, per_group, slot_pad, sub), F32),
                pltpu.VMEM((N_SUB, n_grp, n_loc * tok, sub), BF16),
                pltpu.VMEM((N_SUB, n_grp, n_loc * tok, sub), BF16),
                pltpu.VMEM((N_SUB, n_loc, tok, sub), BF16),
                pltpu.VMEM((N_SUB, n_loc, tok, sub), BF16),
                dma((n_exp, 2 + n_loc)),
                dma((n_loc,)), dma((n_loc,)),
                dma((n_grp,)), dma((n_grp,)),
                dma((N_CHUNK, 4)), dma((N_CHUNK, 4)),
                dma((N_CHUNK, 4)), dma((N_CHUNK, 4)),
                dma((N_CHUNK, 4)), dma((N_CHUNK, 4)),
                dma((n_exp, N_SUB, n_loc)), dma((n_exp, N_SUB, n_loc)),
                dma((N_SUB, n_grp)), dma((N_SUB, n_grp)),
                dma((N_SUB, n_loc)), dma((N_SUB, n_loc)),
            ],
            compiler_params=pltpu.CompilerParams(collective_id=0, has_side_effects=True, vmem_limit_bytes=64000 * 1024),
        )(x_tok, expert_ids.T, gate_val.T, w_gate, w_up, w_down)

    return jax.shard_map(device_step, mesh=mesh, in_specs=(tok_spec, tok_spec, tok_spec, w_spec, w_spec, w_spec), out_specs=tok_spec, check_vma=False)
```

time: 62.8 us -> 58 us (0.924)
  local copies, waits for them, and re-layouts: 4.19 us -> 1.47 us
  Pallas kernels: 58.3 us -> 56.4 us
    unnamed x3 -> x1, local copies, waits for them, and re-layouts: 4.19 us -> 1.47 us
    pallas_call x1, Pallas kernels: 58.3 us -> 56.4 us  [device_step(): pl.pallas_call(functools.partial(layer_kernel, n_loc, n_grp, cap, top_k),...]
where the time goes in v2:
time: 58 us; the launch traced here: 57.8 us
  Pallas kernels  56.4 us (97%)
  local copies, waits for them, and re-layouts  1.47 us (3%)
    pallas_call x1, Pallas kernels, device_step(): pl.pallas_call(functools.partial(layer_kernel, n_loc, n_grp, cap, top_k),...  56.4 us
    unnamed x1, local copies, waits for them, and re-layouts  1.47 us

profile of v2, /device:TPU:97, one launch (start us, length us, event | category | flops | bytes accessed | tf_op | source)
XLA Modules:
  0.0 57.8 jit_solution(15543262572457228668)
XLA Ops:
  0.0 56.4 %shard_map.64 = bf16[16,2048]{1,0:T(8,128)(2,1)} custom-call(bf16[16,2048]{1,0:T(8,128)(2,1)} %x_ref.1, s32[6,16]{1,0:T(8,128)} %bitcast.2, f32[6,16]{1,0:T(8,128)} %bitcast.3, bf16[2,2048,1408]{2,1,0:T(8,128)(2,1)} %wg_hbm.1, bf16[2,2048,1408]{2,1,0:T(8,128)(2,1)} %wu_hbm.1, bf16[2,1408,2048]{2,1,0:T(8,128)(2,1)} %wd_hbm.1), custom_call_target="tpu_custom_call" | custom-call | tf_op jit(solution)/shard_map/pallas_call | solution.py:254
  56.4 1.5 %copy.8 = bf16[16,2048]{1,0:T(8,128)(2,1)} copy(bf16[16,2048]{1,0:T(8,128)(2,1)} %shard_map.64) | data formatting | bytes 131072

commit v3 on v2

v3 whole, which is shorter than its diff:
```python
import functools

import jax
import jax.numpy as jnp
from jax import lax
from jax.experimental import pallas as pl
from jax.experimental.pallas import tpu as pltpu
from jax.sharding import PartitionSpec as P

MESH = pl.DeviceIdType.MESH
F32, BF16 = jnp.float32, jnp.bfloat16
N_SUB = 4
N_CHUNK = 4


def remote(src, dst, send_sem, recv_sem, device):
    return pltpu.make_async_remote_copy(src_ref=src, dst_ref=dst, send_sem=send_sem, recv_sem=recv_sem, device_id=device, device_id_type=MESH)


def drain(ref, sem):
    pltpu.make_async_copy(ref, ref, sem).wait()


def layer_kernel(n_loc, n_grp, cap, top_k, x_ref, ids_ref, gate_ref, wg_hbm, wu_hbm, wd_hbm, out_ref,
                 wg, wu, wd, xall, mown, mcol, mrow, mall, tri, picks, xg, uacc, vacc, hid, combine, ysend, yrecv, gpart, grecv, fin, frecv,
                 w_sem, m_send, m_recv, a_send, a_recv, b_send, b_recv, s_send, s_recv,
                 y_send, y_recv, g_send, g_recv, f_send, f_recv):
    n_x = n_grp // 2
    tok, d_model = x_ref.shape
    width = d_model // N_CHUNK
    n_exp, _, d_ff = wg.shape
    per_group = n_exp * n_loc
    quarter = d_model // n_loc
    sub = quarter // N_SUB
    n_tok = n_grp * n_loc * tok
    slot_pad = yrecv.shape[2]
    cap_pad = hid.shape[1]

    l, g = lax.axis_index("loc"), lax.axis_index("grp")
    gx, gc = g // 2, g % 2

    def at_y(d):
        return (l + d + n_loc) % n_loc

    def at_x(d):
        return (gx + d + n_x) % n_x

    def at_g(d):
        return (g + d + n_grp) % n_grp

    def dev_y(d):
        return {"loc": at_y(d), "grp": g}

    def dev_x(d):
        return {"loc": l, "grp": at_x(d) * 2 + gc}

    def dev_g(d):
        return {"loc": l, "grp": at_g(d)}

    sibling = {"loc": l, "grp": gx * 2 + 1 - gc}

    barrier = pltpu.get_barrier_semaphore()
    for d in range(1, n_loc):
        pl.semaphore_signal(barrier, inc=1, device_id=dev_y(d), device_id_type=MESH)
    for d in range(1, n_grp):
        pl.semaphore_signal(barrier, inc=1, device_id=dev_g(d), device_id_type=MESH)

    loads = {}
    for e in range(n_exp):
        for j, (src, dst) in enumerate(((wg_hbm, wg), (wu_hbm, wu))):
            loads[e, j] = pltpu.make_async_copy(src.at[e], dst.at[e], w_sem.at[e, j])
            loads[e, j].start()
    for e in range(n_exp):
        for d in (2, 1, 3, 0):
            cols = pl.ds(pl.multiple_of(at_y(d) * quarter, quarter), quarter)
            loads[e, 2 + d] = pltpu.make_async_copy(wd_hbm.at[e, :, cols], wd.at[e, d], w_sem.at[e, 2])
            loads[e, 2 + d].start()

    lanes = n_loc * tok
    mown[...] = jnp.zeros(mown.shape, F32)
    mown[0:top_k, 0:tok] = ids_ref[...].astype(F32)
    mown[0:top_k, lanes:lanes + tok] = gate_ref[...]
    mown[...] = pltpu.roll(mown[...], l * tok, 1)
    xall[gx, gc, l] = x_ref[...]
    tri_r = lax.broadcasted_iota(jnp.int32, (n_tok, n_tok), 0)
    tri_c = lax.broadcasted_iota(jnp.int32, (n_tok, n_tok), 1)
    tri[...] = jnp.where(tri_r < tri_c, 1.0, 0.0).astype(BF16)
    yrecv[:, :, cap:, :] = jnp.zeros((N_SUB, per_group, slot_pad - cap, sub), F32)

    pl.semaphore_wait(barrier, n_loc + n_grp - 2)

    def go(copy):
        copy.start()

    far_first, near_first = (2, 1, 3), (1, 3, 2)
    for d in far_first:
        go(remote(mown, mcol.at[d], m_send, m_recv.at[0], dev_y(d)))

    def half(p):
        return pl.ds(p * 2 * width, 2 * width)

    for p in range(2):
        for d in far_first:
            for axis in range(2):
                go(remote(x_ref.at[:, half(p)], xall.at[gx, gc, l, :, half(p)], a_send, a_recv.at[axis, p, d - 1], dev_x(d) if axis else dev_y(d)))
    drain(mcol.at[pl.ds(1, n_loc - 1)], m_recv.at[0])
    mrow[...] = mown[...] + mcol[1] + mcol[2] + mcol[3]
    mall[gx, gc] = mrow[...]
    for d in far_first:
        go(remote(mrow, mall.at[gx, gc], m_send, m_recv.at[1], dev_x(d)))
    go(remote(mrow, mall.at[gx, gc], m_send, m_recv.at[2], sibling))

    def relay(p, d):
        part = xall.at[at_x(-d), gc, :, :, half(p)]
        go(remote(part, part, s_send, s_recv.at[p], sibling))

    for p in range(2):
        for d in near_first:
            for axis in range(2):
                drain(xall.at[at_x(-d), gc, l, :, half(p)] if axis else xall.at[gx, gc, at_y(-d), :, half(p)], a_recv.at[axis, p, d - 1])
                cols = pl.ds((2 * p + axis) * width, width)
                part = xall.at[at_x(-d), gc, l, :, cols] if axis else xall.at[gx, gc, at_y(-d), :, cols]
                for t in far_first:
                    go(remote(part, part, b_send, b_recv.at[p, (d if axis else t) - 1], dev_y(t) if axis else dev_x(t)))
        relay(p, 0)
        if p == 0:
            drain(mall.at[pl.ds(0, n_x - 1), 0], m_recv.at[1])
            for d in near_first:
                part = mall.at[at_x(-d), gc]
                go(remote(part, part, m_send, m_recv.at[2], sibling))

    drain(mall.at[:, 0], m_recv.at[2])
    lane = lax.broadcasted_iota(jnp.int32, mall.shape[2:], 1)
    ids = jnp.concatenate([jnp.where(lane < lanes, mall[i, 0], pltpu.roll(mall[i, 1], lanes, 1)) for i in range(n_x)], axis=1)
    gate_of = jnp.concatenate([jnp.where(lane < lanes, pltpu.roll(mall[i, 0], lanes, 1), mall[i, 1]) for i in range(n_x)], axis=1)
    row = lax.broadcasted_iota(jnp.int32, (per_group, n_tok), 0)
    row_exp = (g * per_group + ((l + n_loc - row // n_exp) % n_loc) * n_exp + row % n_exp).astype(F32)
    member = jnp.zeros(row.shape, F32)
    gates = jnp.zeros(row.shape, F32)
    for j in range(top_k):
        same = ids[j:j + 1, :] == row_exp
        member = jnp.where(same, 1.0, member)
        gates = jnp.where(same, gate_of[j:j + 1, :], gates)
    before = jnp.dot(member.astype(BF16), tri[...], preferred_element_type=F32)
    slot = jnp.where(member > 0.0, before, -1.0)
    cap_row = lax.broadcasted_iota(jnp.int32, (cap_pad, n_tok), 0).astype(F32)
    slot_gate = []
    for e in range(n_exp):
        hit = cap_row == slot[e:e + 1, :]
        picks[e * cap_pad:(e + 1) * cap_pad, :] = jnp.where(hit, 1.0, 0.0).astype(BF16)
        slot_gate.append(jnp.sum(jnp.where(hit, gates[e:e + 1, :], 0.0), axis=1, keepdims=True))

    tile = min(256, d_ff)
    tiles = [(c0, min(d_ff, c0 + tile)) for c0 in range(0, d_ff, tile)]
    for p in range(2):
        for d in near_first:
            drain(xall.at[at_x(-d), gc, pl.ds(0, n_loc - 1), :, half(p)], b_recv.at[p, d - 1])
            relay(p, d)
        drain(xall.at[:, 1 - gc, :, :, half(p)], s_recv.at[p])
        for h in (2 * p, 2 * p + 1):
            rows = xall[:, :, :, :, h * width:(h + 1) * width].reshape(n_tok, width)
            got = jnp.dot(picks[...], rows, preferred_element_type=F32).astype(BF16)
            for e in range(n_exp):
                xg[e, :, h * width:(h + 1) * width] = got[e * cap_pad:(e + 1) * cap_pad]
        k0, k1 = 2 * p * width, 2 * (p + 1) * width
        if p == 0:
            for e in range(n_exp):
                loads[e, 0].wait()
                loads[e, 1].wait()
                for c0, c1 in tiles:
                    uacc[e, :, c0:c1] = jnp.dot(xg[e, :, k0:k1], wg[e, k0:k1, c0:c1], preferred_element_type=F32)
                    vacc[e, :, c0:c1] = jnp.dot(xg[e, :, k0:k1], wu[e, k0:k1, c0:c1], preferred_element_type=F32)
    for e in range(n_exp):
        for c0, c1 in tiles:
            u = uacc[e, :, c0:c1] + jnp.dot(xg[e, :, k0:k1], wg[e, k0:k1, c0:c1], preferred_element_type=F32)
            v = vacc[e, :, c0:c1] + jnp.dot(xg[e, :, k0:k1], wu[e, k0:k1, c0:c1], preferred_element_type=F32)
            hid[e, :, c0:c1] = (jax.nn.silu(u) * v).astype(BF16)

        def send_rows(e, k, d):
            go(remote(ysend.at[d - 1, e, k, pl.ds(0, cap)], yrecv.at[k, n_exp * d + e, pl.ds(0, cap)], y_send, y_recv.at[k], dev_y(d)))

        drain(wd.at[e], w_sem.at[e, 2])
        for d in far_first:
            o = jnp.dot(hid[e], wd[e, d], preferred_element_type=F32) * slot_gate[e]
            for k in range(N_SUB):
                ysend[d - 1, e, k] = o[:, k * sub:(k + 1) * sub]
            if e + 1 < n_exp:
                for k in range(N_SUB):
                    send_rows(e, k, d)
        if e + 1 == n_exp:
            for k in range(N_SUB):
                for d in far_first:
                    send_rows(e, k, d)
    for e in range(n_exp):
        o = jnp.dot(hid[e], wd[e, 0], preferred_element_type=F32) * slot_gate[e]
        for k in range(N_SUB):
            yrecv[k, e, 0:cap, :] = o[0:cap, k * sub:(k + 1) * sub]
    slot_cols = jnp.transpose(jnp.concatenate([slot, jnp.zeros((128 - per_group, n_tok), F32)], axis=0))
    slot_lane = lax.broadcasted_iota(jnp.int32, (n_tok, slot_pad), 1).astype(F32)
    for i in range(per_group):
        combine[:, i * slot_pad:(i + 1) * slot_pad] = jnp.where(slot_lane == slot_cols[:, i:i + 1], 1.0, 0.0).astype(BF16)

    for k in range(N_SUB):
        drain(yrecv.at[k, pl.ds(n_exp, per_group - n_exp), pl.ds(0, cap)], y_recv.at[k])
        vals = yrecv[k].reshape(per_group * slot_pad, sub)
        hi = vals.astype(BF16)
        rest = vals - hi.astype(F32)
        mid = rest.astype(BF16)
        low = (rest - mid.astype(F32)).astype(BF16)
        sel = combine[...]
        both = jnp.dot(sel, jnp.concatenate([hi, mid], axis=1), preferred_element_type=F32)
        acc = both[:, 0:sub] + both[:, sub:] + jnp.dot(sel, low, preferred_element_type=F32)
        gpart[k] = acc.astype(BF16).reshape(n_grp, n_loc * tok, sub)
        for d in (4, 3, 5, 2, 6, 1, 7):
            go(remote(gpart.at[k, at_g(d)], grecv.at[k, d], g_send, g_recv.at[k], dev_g(d)))

    for k in range(N_SUB):
        total = gpart[k, g].astype(F32)
        drain(grecv.at[k, pl.ds(1, n_grp - 1)], g_recv.at[k])
        for d in range(1, n_grp):
            total += grecv[k, d].astype(F32)
        fin[k] = total.astype(BF16).reshape(n_loc, tok, sub)
        for d in far_first:
            go(remote(fin.at[k, at_y(d)], frecv.at[k, d], f_send, f_recv, dev_y(d)))
    drain(frecv.at[:, pl.ds(1, n_loc - 1)], f_recv)
    for k in range(N_SUB):
        for d in range(n_loc):
            cols = pl.ds(pl.multiple_of(at_y(-d) * quarter + k * sub, sub), sub)
            out_ref[:, cols] = frecv[k, d] if d else fin[k, l]
    drain(ysend.at[0, 0, 0, pl.ds(0, 8 * (2 * n_loc + 2))], m_send)
    drain(xall.at[pl.ds(0, 3), 0, pl.ds(0, 4), :, half(0)], a_send)
    drain(xall.at[pl.ds(0, 3), :, pl.ds(0, 3), :, half(0)], b_send)
    drain(xall.at[:, 0], s_send)
    drain(ysend.at[:, :, :, pl.ds(0, cap)], y_send)
    drain(grecv.at[:, pl.ds(1, n_grp - 1)], g_send)
    drain(frecv.at[:, pl.ds(1, n_loc - 1)], f_send)


def solution(mesh):
    n_grp, n_loc = mesh.shape["grp"], mesh.shape["loc"]
    tok_spec = P(("part", "grp", "loc"), None)
    w_spec = P(("grp", "loc"), None, None)

    def device_step(x_tok, expert_ids, gate_val, w_gate, w_up, w_down):
        tok, d_model = x_tok.shape
        top_k = expert_ids.shape[1]
        n_exp, _, d_ff = w_gate.shape
        n_tok = tok * n_grp * n_loc
        per_group = n_exp * n_loc
        cap = 8 * (n_tok * top_k // (4 * per_group * n_grp) + 1)
        slot_pad = -(-cap // 128) * 128
        cap_pad = -(-cap // 16) * 16
        quarter = d_model // n_loc
        sub = quarter // N_SUB
        dma = pltpu.SemaphoreType.DMA
        vmem = pl.BlockSpec(memory_space=pltpu.VMEM)
        hbm = pl.BlockSpec(memory_space=pl.ANY)
        return pl.pallas_call(
            functools.partial(layer_kernel, n_loc, n_grp, cap, top_k),
            out_shape=jax.ShapeDtypeStruct((tok, d_model), BF16),
            in_specs=[vmem, vmem, vmem, hbm, hbm, hbm],
            out_specs=vmem,
            scratch_shapes=[
                pltpu.VMEM((n_exp, d_model, d_ff), BF16),
                pltpu.VMEM((n_exp, d_model, d_ff), BF16),
                pltpu.VMEM((n_exp, n_loc, d_ff, quarter), BF16),
                pltpu.VMEM((n_grp // 2, 2, n_loc, tok, d_model), BF16),
                pltpu.VMEM((8, 128), F32),
                pltpu.VMEM((n_loc, 8, 128), F32),
                pltpu.VMEM((8, 128), F32),
                pltpu.VMEM((n_grp // 2, 2, 8, 128), F32),
                pltpu.VMEM((n_tok, n_tok), BF16),
                pltpu.VMEM((n_exp * cap_pad, n_tok), BF16),
                pltpu.VMEM((n_exp, cap_pad, d_model), BF16),
                pltpu.VMEM((n_exp, cap_pad, d_ff), F32),
                pltpu.VMEM((n_exp, cap_pad, d_ff), F32),
                pltpu.VMEM((n_exp, cap_pad, d_ff), BF16),
                pltpu.VMEM((n_tok, per_group * slot_pad), BF16),
                pltpu.VMEM((n_loc - 1, n_exp, N_SUB, cap_pad, sub), F32),
                pltpu.VMEM((N_SUB, per_group, slot_pad, sub), F32),
                pltpu.VMEM((N_SUB, n_grp, n_loc * tok, sub), BF16),
                pltpu.VMEM((N_SUB, n_grp, n_loc * tok, sub), BF16),
                pltpu.VMEM((N_SUB, n_loc, tok, sub), BF16),
                pltpu.VMEM((N_SUB, n_loc, tok, sub), BF16),
                dma((n_exp, 3)),
                dma, dma((3,)),
                dma, dma((2, 2, 3)),
                dma, dma((2, 3)),
                dma, dma((2,)),
                dma, dma((N_SUB,)),
                dma, dma((N_SUB,)),
                dma, dma,
            ],
            compiler_params=pltpu.CompilerParams(collective_id=0, has_side_effects=True, vmem_limit_bytes=64000 * 1024),
        )(x_tok, expert_ids.T, gate_val.T, w_gate, w_up, w_down)

    return jax.shard_map(device_step, mesh=mesh, in_specs=(tok_spec, tok_spec, tok_spec, w_spec, w_spec, w_spec), out_specs=tok_spec, check_vma=False)
```

time: 58 us -> 53.8 us (0.928)
  Pallas kernels: 56.4 us -> 52.1 us
    pallas_call x1, Pallas kernels: 56.4 us -> 52.1 us  [device_step(): pl.pallas_call(functools.partial(layer_kernel, n_loc, n_grp, cap, top_k),...]
where the time goes in v3:
time: 53.8 us; the launch traced here: 53.6 us
  Pallas kernels  52.1 us (97%)
  local copies, waits for them, and re-layouts  1.47 us (3%)
    pallas_call x1, Pallas kernels, device_step(): pl.pallas_call(functools.partial(layer_kernel, n_loc, n_grp, cap, top_k),...  52.1 us
    unnamed x1, local copies, waits for them, and re-layouts  1.47 us

profile of v3, /device:TPU:97, one launch (start us, length us, event | category | flops | bytes accessed | tf_op | source)
XLA Modules:
  0.0 53.6 jit_solution(6888216792529726294)
XLA Ops:
  0.0 52.1 %shard_map.64 = bf16[16,2048]{1,0:T(8,128)(2,1)} custom-call(bf16[16,2048]{1,0:T(8,128)(2,1)} %x_ref.1, s32[6,16]{1,0:T(8,128)} %bitcast.2, f32[6,16]{1,0:T(8,128)} %bitcast.3, bf16[2,2048,1408]{2,1,0:T(8,128)(2,1)} %wg_hbm.1, bf16[2,2048,1408]{2,1,0:T(8,128)(2,1)} %wu_hbm.1, bf16[2,1408,2048]{2,1,0:T(8,128)(2,1)} %wd_hbm.1), custom_call_target="tpu_custom_call" | custom-call | tf_op jit(solution)/shard_map/pallas_call | solution.py:258
  52.1 1.5 %copy.8 = bf16[16,2048]{1,0:T(8,128)(2,1)} copy(bf16[16,2048]{1,0:T(8,128)(2,1)} %shard_map.64) | data formatting | bytes 131072

commit v4 on v3

--- a/solution.py
+++ b/solution.py
@@ -21,9 +21,9 @@
     pltpu.make_async_copy(ref, ref, sem).wait()
 
 
-def layer_kernel(n_loc, n_grp, cap, top_k, x_ref, ids_ref, gate_ref, wg_hbm, wu_hbm, wd_hbm, out_ref,
-                 wg, wu, wd, xall, mown, mcol, mrow, mall, tri, picks, xg, uacc, vacc, hid, combine, ysend, yrecv, gpart, grecv, fin, frecv,
-                 w_sem, m_send, m_recv, a_send, a_recv, b_send, b_recv, s_send, s_recv,
+def layer_kernel(n_loc, n_grp, cap, top_k, x_hbm, ids_hbm, gate_hbm, wg_hbm, wu_hbm, wd_hbm, out_ref,
+                 x_ref, ids_ref, gate_ref, wg, wu, wd, xall, mown, mcol, mrow, mall, tri, picks, xg, uacc, vacc, hid, combine, ysend, yrecv, gpart, grecv, fin, frecv,
+                 i_sem, w_sem, m_send, m_recv, a_send, a_recv, b_send, b_recv, s_send, s_recv,
                  y_send, y_recv, g_send, g_recv, f_send, f_recv):
     n_x = n_grp // 2
     tok, d_model = x_ref.shape
@@ -65,6 +65,16 @@
     for d in range(1, n_grp):
         pl.semaphore_signal(barrier, inc=1, device_id=dev_g(d), device_id_type=MESH)
 
+    inputs = [pltpu.make_async_copy(src, dst, i_sem.at[i]) for i, (src, dst) in enumerate(((ids_hbm, ids_ref), (gate_hbm, gate_ref), (x_hbm, x_ref)))]
+    for c in inputs:
+        c.start()
+
+    tri_r = lax.broadcasted_iota(jnp.int32, (n_tok, n_tok), 0)
+    tri_c = lax.broadcasted_iota(jnp.int32, (n_tok, n_tok), 1)
+    tri[...] = jnp.where(tri_r < tri_c, 1.0, 0.0).astype(BF16)
+    yrecv[:, :, cap:, :] = jnp.zeros((N_SUB, per_group, slot_pad - cap, sub), F32)
+    for c in inputs:
+        c.wait()
     loads = {}
     for e in range(n_exp):
         for j, (src, dst) in enumerate(((wg_hbm, wg), (wu_hbm, wu))):
@@ -82,10 +92,6 @@
     mown[0:top_k, lanes:lanes + tok] = gate_ref[...]
     mown[...] = pltpu.roll(mown[...], l * tok, 1)
     xall[gx, gc, l] = x_ref[...]
-    tri_r = lax.broadcasted_iota(jnp.int32, (n_tok, n_tok), 0)
-    tri_c = lax.broadcasted_iota(jnp.int32, (n_tok, n_tok), 1)
-    tri[...] = jnp.where(tri_r < tri_c, 1.0, 0.0).astype(BF16)
-    yrecv[:, :, cap:, :] = jnp.zeros((N_SUB, per_group, slot_pad - cap, sub), F32)
 
     pl.semaphore_wait(barrier, n_loc + n_grp - 2)
 
@@ -164,16 +170,23 @@
                 xg[e, :, h * width:(h + 1) * width] = got[e * cap_pad:(e + 1) * cap_pad]
         k0, k1 = 2 * p * width, 2 * (p + 1) * width
         if p == 0:
-            for e in range(n_exp):
+            for e in range(1):
                 loads[e, 0].wait()
                 loads[e, 1].wait()
                 for c0, c1 in tiles:
-                    uacc[e, :, c0:c1] = jnp.dot(xg[e, :, k0:k1], wg[e, k0:k1, c0:c1], preferred_element_type=F32)
-                    vacc[e, :, c0:c1] = jnp.dot(xg[e, :, k0:k1], wu[e, k0:k1, c0:c1], preferred_element_type=F32)
-    for e in range(n_exp):
+                    uacc[:, c0:c1] = jnp.dot(xg[e, :, k0:k1], wg[e, k0:k1, c0:c1], preferred_element_type=F32)
+                    vacc[:, c0:c1] = jnp.dot(xg[e, :, k0:k1], wu[e, k0:k1, c0:c1], preferred_element_type=F32)
+    for e in range(n_exp):
+        if e:
+            loads[e, 0].wait()
+            loads[e, 1].wait()
         for c0, c1 in tiles:
-            u = uacc[e, :, c0:c1] + jnp.dot(xg[e, :, k0:k1], wg[e, k0:k1, c0:c1], preferred_element_type=F32)
-            v = vacc[e, :, c0:c1] + jnp.dot(xg[e, :, k0:k1], wu[e, k0:k1, c0:c1], preferred_element_type=F32)
+            if e:
+                u = jnp.dot(xg[e], wg[e, :, c0:c1], preferred_element_type=F32)
+                v = jnp.dot(xg[e], wu[e, :, c0:c1], preferred_element_type=F32)
+            else:
+                u = uacc[:, c0:c1] + jnp.dot(xg[e, :, k0:k1], wg[e, k0:k1, c0:c1], preferred_element_type=F32)
+                v = vacc[:, c0:c1] + jnp.dot(xg[e, :, k0:k1], wu[e, k0:k1, c0:c1], preferred_element_type=F32)
             hid[e, :, c0:c1] = (jax.nn.silu(u) * v).astype(BF16)
 
         def send_rows(e, k, d):
@@ -258,9 +271,12 @@
         return pl.pallas_call(
             functools.partial(layer_kernel, n_loc, n_grp, cap, top_k),
             out_shape=jax.ShapeDtypeStruct((tok, d_model), BF16),
-            in_specs=[vmem, vmem, vmem, hbm, hbm, hbm],
+            in_specs=[hbm] * 6,
             out_specs=vmem,
             scratch_shapes=[
+                pltpu.VMEM((tok, d_model), BF16),
+                pltpu.VMEM((top_k, tok), jnp.int32),
+                pltpu.VMEM((top_k, tok), F32),
                 pltpu.VMEM((n_exp, d_model, d_ff), BF16),
                 pltpu.VMEM((n_exp, d_model, d_ff), BF16),
                 pltpu.VMEM((n_exp, n_loc, d_ff, quarter), BF16),
@@ -272,8 +288,8 @@
                 pltpu.VMEM((n_tok, n_tok), BF16),
                 pltpu.VMEM((n_exp * cap_pad, n_tok), BF16),
                 pltpu.VMEM((n_exp, cap_pad, d_model), BF16),
-                pltpu.VMEM((n_exp, cap_pad, d_ff), F32),
-                pltpu.VMEM((n_exp, cap_pad, d_ff), F32),
+                pltpu.VMEM((cap_pad, d_ff), F32),
+                pltpu.VMEM((cap_pad, d_ff), F32),
                 pltpu.VMEM((n_exp, cap_pad, d_ff), BF16),
                 pltpu.VMEM((n_tok, per_group * slot_pad), BF16),
                 pltpu.VMEM((n_loc - 1, n_exp, N_SUB, cap_pad, sub), F32),
@@ -282,6 +298,7 @@
                 pltpu.VMEM((N_SUB, n_grp, n_loc * tok, sub), BF16),
                 pltpu.VMEM((N_SUB, n_loc, tok, sub), BF16),
                 pltpu.VMEM((N_SUB, n_loc, tok, sub), BF16),
+                dma((3,)),
                 dma((n_exp, 3)),
                 dma, dma((3,)),
                 dma, dma((2, 2, 3)),

time: 53.8 us -> 52 us (0.967)
  Pallas kernels: 52.1 us -> 50.3 us
    pallas_call x1, Pallas kernels: 52.1 us -> 50.3 us  [device_step(): pl.pallas_call(functools.partial(layer_kernel, n_loc, n_grp, cap, top_k),...]
where the time goes in v4:
time: 52 us; the launch traced here: 51.8 us
  Pallas kernels  50.3 us (97%)
  local copies, waits for them, and re-layouts  1.47 us (3%)
    pallas_call x1, Pallas kernels, device_step(): pl.pallas_call(functools.partial(layer_kernel, n_loc, n_grp, cap, top_k),...  50.3 us
    unnamed x1, local copies, waits for them, and re-layouts  1.47 us

profile of v4, /device:TPU:97, one launch (start us, length us, event | category | flops | bytes accessed | tf_op | source)
XLA Modules:
  0.0 51.8 jit_solution(7571076063738803012)
XLA Ops:
  0.0 50.3 %shard_map.64 = bf16[16,2048]{1,0:T(8,128)(2,1)} custom-call(bf16[16,2048]{1,0:T(8,128)(2,1)} %x_hbm.1, s32[6,16]{1,0:T(8,128)} %bitcast.2, f32[6,16]{1,0:T(8,128)} %bitcast.3, bf16[2,2048,1408]{2,1,0:T(8,128)(2,1)} %wg_hbm.1, bf16[2,2048,1408]{2,1,0:T(8,128)(2,1)} %wu_hbm.1, bf16[2,1408,2048]{2,1,0:T(8,128)(2,1)} %wd_hbm.1), custom_call_target="tpu_custom_call" | custom-call | tf_op jit(solution)/shard_map/pallas_call | solution.py:271
  50.3 1.5 %copy.8 = bf16[16,2048]{1,0:T(8,128)(2,1)} copy(bf16[16,2048]{1,0:T(8,128)(2,1)} %shard_map.64) | data formatting | bytes 131072

commit v5 on v4

--- a/solution.py
+++ b/solution.py
@@ -22,7 +22,7 @@
 
 
 def layer_kernel(n_loc, n_grp, cap, top_k, x_hbm, ids_hbm, gate_hbm, wg_hbm, wu_hbm, wd_hbm, out_ref,
-                 x_ref, ids_ref, gate_ref, wg, wu, wd, xall, mown, mcol, mrow, mall, tri, picks, xg, uacc, vacc, hid, combine, ysend, yrecv, gpart, grecv, fin, frecv,
+                 x_ref, ids_ref, gate_ref, wg, wu, wd, xall, mown, mcol, mrow, mall, tri, picks, xg, uacc, vacc, hid, combine, partial, ysend, yrecv, gpart, grecv, fin, frecv,
                  i_sem, w_sem, m_send, m_recv, a_send, a_recv, b_send, b_recv, s_send, s_recv,
                  y_send, y_recv, g_send, g_recv, f_send, f_recv):
     n_x = n_grp // 2
@@ -140,7 +140,7 @@
     ids = jnp.concatenate([jnp.where(lane < lanes, mall[i, 0], pltpu.roll(mall[i, 1], lanes, 1)) for i in range(n_x)], axis=1)
     gate_of = jnp.concatenate([jnp.where(lane < lanes, pltpu.roll(mall[i, 0], lanes, 1), mall[i, 1]) for i in range(n_x)], axis=1)
     row = lax.broadcasted_iota(jnp.int32, (per_group, n_tok), 0)
-    row_exp = (g * per_group + ((l + n_loc - row // n_exp) % n_loc) * n_exp + row % n_exp).astype(F32)
+    row_exp = (g * per_group + ((l + n_loc - row % n_loc) % n_loc) * n_exp + row // n_loc).astype(F32)
     member = jnp.zeros(row.shape, F32)
     gates = jnp.zeros(row.shape, F32)
     for j in range(top_k):
@@ -152,9 +152,9 @@
     cap_row = lax.broadcasted_iota(jnp.int32, (cap_pad, n_tok), 0).astype(F32)
     slot_gate = []
     for e in range(n_exp):
-        hit = cap_row == slot[e:e + 1, :]
+        hit = cap_row == slot[e * n_loc:e * n_loc + 1, :]
         picks[e * cap_pad:(e + 1) * cap_pad, :] = jnp.where(hit, 1.0, 0.0).astype(BF16)
-        slot_gate.append(jnp.sum(jnp.where(hit, gates[e:e + 1, :], 0.0), axis=1, keepdims=True))
+        slot_gate.append(jnp.sum(jnp.where(hit, gates[e * n_loc:e * n_loc + 1, :], 0.0), axis=1, keepdims=True))
 
     tile = min(256, d_ff)
     tiles = [(c0, min(d_ff, c0 + tile)) for c0 in range(0, d_ff, tile)]
@@ -190,7 +190,7 @@
             hid[e, :, c0:c1] = (jax.nn.silu(u) * v).astype(BF16)
 
         def send_rows(e, k, d):
-            go(remote(ysend.at[d - 1, e, k, pl.ds(0, cap)], yrecv.at[k, n_exp * d + e, pl.ds(0, cap)], y_send, y_recv.at[k], dev_y(d)))
+            go(remote(ysend.at[d - 1, e, k, pl.ds(0, cap)], yrecv.at[k, n_loc * e + d, pl.ds(0, cap)], y_send, y_recv.at[e, k], dev_y(d)))
 
         drain(wd.at[e], w_sem.at[e, 2])
         for d in far_first:
@@ -207,22 +207,29 @@
     for e in range(n_exp):
         o = jnp.dot(hid[e], wd[e, 0], preferred_element_type=F32) * slot_gate[e]
         for k in range(N_SUB):
-            yrecv[k, e, 0:cap, :] = o[0:cap, k * sub:(k + 1) * sub]
+            yrecv[k, n_loc * e, 0:cap, :] = o[0:cap, k * sub:(k + 1) * sub]
     slot_cols = jnp.transpose(jnp.concatenate([slot, jnp.zeros((128 - per_group, n_tok), F32)], axis=0))
     slot_lane = lax.broadcasted_iota(jnp.int32, (n_tok, slot_pad), 1).astype(F32)
     for i in range(per_group):
         combine[:, i * slot_pad:(i + 1) * slot_pad] = jnp.where(slot_lane == slot_cols[:, i:i + 1], 1.0, 0.0).astype(BF16)
 
-    for k in range(N_SUB):
-        drain(yrecv.at[k, pl.ds(n_exp, per_group - n_exp), pl.ds(0, cap)], y_recv.at[k])
-        vals = yrecv[k].reshape(per_group * slot_pad, sub)
+    def token_sums(e, k):
+        drain(yrecv.at[k, pl.ds(n_loc * e + 1, n_loc - 1), pl.ds(0, cap)], y_recv.at[e, k])
+        vals = yrecv[k, n_loc * e:n_loc * (e + 1)].reshape(n_loc * slot_pad, sub)
         hi = vals.astype(BF16)
         rest = vals - hi.astype(F32)
         mid = rest.astype(BF16)
         low = (rest - mid.astype(F32)).astype(BF16)
-        sel = combine[...]
+        sel = combine[:, e * n_loc * slot_pad:(e + 1) * n_loc * slot_pad]
         both = jnp.dot(sel, jnp.concatenate([hi, mid], axis=1), preferred_element_type=F32)
-        acc = both[:, 0:sub] + both[:, sub:] + jnp.dot(sel, low, preferred_element_type=F32)
+        return both[:, 0:sub] + both[:, sub:] + jnp.dot(sel, low, preferred_element_type=F32)
+
+    for k in range(N_SUB):
+        partial[k] = token_sums(0, k)
+    for k in range(N_SUB):
+        acc = partial[k]
+        for e in range(1, n_exp):
+            acc += token_sums(e, k)
         gpart[k] = acc.astype(BF16).reshape(n_grp, n_loc * tok, sub)
         for d in (4, 3, 5, 2, 6, 1, 7):
             go(remote(gpart.at[k, at_g(d)], grecv.at[k, d], g_send, g_recv.at[k], dev_g(d)))
@@ -292,6 +299,7 @@
                 pltpu.VMEM((cap_pad, d_ff), F32),
                 pltpu.VMEM((n_exp, cap_pad, d_ff), BF16),
                 pltpu.VMEM((n_tok, per_group * slot_pad), BF16),
+                pltpu.VMEM((N_SUB, n_tok, sub), F32),
                 pltpu.VMEM((n_loc - 1, n_exp, N_SUB, cap_pad, sub), F32),
                 pltpu.VMEM((N_SUB, per_group, slot_pad, sub), F32),
                 pltpu.VMEM((N_SUB, n_grp, n_loc * tok, sub), BF16),
@@ -304,7 +312,7 @@
                 dma, dma((2, 2, 3)),
                 dma, dma((2, 3)),
                 dma, dma((2,)),
-                dma, dma((N_SUB,)),
+                dma, dma((n_exp, N_SUB)),
                 dma, dma((N_SUB,)),
                 dma, dma,
             ],

time: 52 us -> 51.7 us (level)
  no operation moved by 1% of the time
where the time goes in v5:
time: 51.7 us; the launch traced here: 51.6 us
  Pallas kernels  50.1 us (97%)
  local copies, waits for them, and re-layouts  1.47 us (3%)
    pallas_call x1, Pallas kernels, device_step(): pl.pallas_call(functools.partial(layer_kernel, n_loc, n_grp, cap, top_k),...  50.1 us
    unnamed x1, local copies, waits for them, and re-layouts  1.47 us

profile of v5, /device:TPU:97, one launch (start us, length us, event | category | flops | bytes accessed | tf_op | source)
XLA Modules:
  0.0 51.6 jit_solution(15461413788036273021)
XLA Ops:
  0.0 50.1 %shard_map.64 = bf16[16,2048]{1,0:T(8,128)(2,1)} custom-call(bf16[16,2048]{1,0:T(8,128)(2,1)} %x_hbm.1, s32[6,16]{1,0:T(8,128)} %bitcast.2, f32[6,16]{1,0:T(8,128)} %bitcast.3, bf16[2,2048,1408]{2,1,0:T(8,128)(2,1)} %wg_hbm.1, bf16[2,2048,1408]{2,1,0:T(8,128)(2,1)} %wu_hbm.1, bf16[2,1408,2048]{2,1,0:T(8,128)(2,1)} %wd_hbm.1), custom_call_target="tpu_custom_call" | custom-call | tf_op jit(solution)/shard_map/pallas_call | solution.py:278
  50.1 1.5 %copy.8 = bf16[16,2048]{1,0:T(8,128)(2,1)} copy(bf16[16,2048]{1,0:T(8,128)(2,1)} %shard_map.64) | data formatting | bytes 131072
